TPU v7x, 128 devices: a whole 4x4x4 slice. The times are simulated.
128 devices in a mesh: sa: 8 (over x, core), an: 16 (over y, z).
Axes of the slice: x: 4, y: 4, z: 4, core: 2. Of those that a mesh axis runs over, the one named last changes fastest.
Arguments:
- decoder_states: bfloat16 [8192, 4096], P('sa', 'an'), may hold values from -170 to 170
- w_query: bfloat16 [4096, 4096], P(None, 'an'), may hold values from -0.09375 to 0.09375
- w_key: bfloat16 [1024, 4096], P(None, 'an'), may hold values from -0.1875 to 0.1875
- w_value: bfloat16 [1024, 4096], P(None, 'an'), may hold values from -0.1875 to 0.1875
- w_out: bfloat16 [4096, 4096], P('an'), may hold values from -0.375 to 0.375
- enc_up: bfloat16 [1024, 4096], replicated, may hold values from -0.1875 to 0.1875
- enc_down: bfloat16 [4096, 1024], replicated, may hold values from -0.09375 to 0.09375
- neighbour_inputs: bfloat16 [1024, 128, 1024], P(('sa', 'an')), may hold values from -6 to 6
- requests: int32 [256], P('sa'), may hold values from 0 to 127, as said below
Outputs:
- cross_output: bfloat16 [8192, 4096], P('sa', 'an')
Inputs may be any that keep to these rules, and one draw needn't show every extreme that they name: Within each block of 32 requests (one index of sa) the owner of a request is its value // 8; no owner receives more than 4 requests of a block and no more than 2 distinct neighbours of one owner are requested in a block; in every block some owner receives exactly 4 requests, 2 of them distinct. A neighbour may be requested several times.
All inputs are finite; a program needn't handle non-finite values.
Results may differ from a plain program's by a relative error of at most 0.01.
The roundings to bfloat16 on the way count: a program that leaves them out, or rounds other values in their place, can miss the bound.
Values may be sent and summed in bfloat16 or wider, within the bound.
A program may use at most 128 MiB of HBM per device.

v0:
```python
import jax
import jax.numpy as jnp
from jax import lax
from jax.sharding import PartitionSpec as P

D = 4096
HEADS = 32
GROUP = 64
NEIGH = 2
EPS = 1e-06


def encode(rows, enc_up, enc_down):
    wide = rows.astype(jnp.float32)
    square = jnp.mean(wide * wide, axis=-1, keepdims=True)
    normed = (wide * lax.rsqrt(square + EPS)).astype(jnp.bfloat16)
    hidden = jax.nn.gelu(
        jnp.dot(normed, enc_up, preferred_element_type=jnp.float32), approximate=False
    ).astype(jnp.bfloat16)
    return (wide + jnp.dot(hidden, enc_down, preferred_element_type=jnp.float32)).astype(
        jnp.bfloat16
    )


def shards(
    decoder_states, w_query, w_key, w_value, w_out, enc_up, enc_down, neighbour_inputs, requests
):
    owner_total = lax.axis_size("an")
    position = lax.axis_index("an")
    tok_rows, local_width = decoder_states.shape
    head_dim = D // HEADS
    heads_here = local_width // head_dim
    scale = float(head_dim) ** (-0.5)
    total_requests = requests.shape[0]
    per_owner = total_requests // owner_total
    nb_own = neighbour_inputs.shape[0]
    span = neighbour_inputs.shape[1]
    owner = requests // nb_own
    local_id = requests % nb_own
    owner_range = jnp.arange(owner_total, dtype=jnp.int32)
    local_range = jnp.arange(nb_own, dtype=jnp.int32)
    hits = (owner[:, None, None] == owner_range[None, :, None]) & (
        local_id[:, None, None] == local_range[None, None, :]
    )
    present = jnp.any(hits, axis=0).astype(jnp.int32)
    ranked = jnp.cumsum(present, axis=1) - present
    slot_of_request = owner * per_owner + ranked[owner, local_id]
    my_present = jnp.sum(jnp.where(owner_range[:, None] == position, present, 0), axis=0)
    my_rank = jnp.sum(jnp.where(owner_range[:, None] == position, ranked, 0), axis=0)
    chosen_mask = (my_present[:, None] == 1) & (
        my_rank[:, None] == jnp.arange(per_owner, dtype=jnp.int32)[None, :]
    )
    local_of_slot = jnp.sum(jnp.where(chosen_mask, local_range[:, None], 0), axis=0)
    rows = w_query
    queries = jnp.dot(
        lax.all_gather(decoder_states, "an", axis=1, tiled=True),
        rows,
        preferred_element_type=jnp.float32,
    )
    chosen = neighbour_inputs[local_of_slot].reshape(per_owner * span, neighbour_inputs.shape[2])
    encoded = encode(chosen, enc_up, enc_down)
    both_weights = jnp.concatenate([w_key, w_value], axis=1)
    projected = jnp.dot(
        lax.all_gather(encoded, "an", axis=0, tiled=True),
        both_weights,
        preferred_element_type=jnp.float32,
    ).astype(jnp.bfloat16)
    projected = projected.reshape(owner_total * per_owner, span, 2 * local_width)
    groups = tok_rows // GROUP
    selected = projected[slot_of_request].reshape(groups, NEIGH * span, 2 * local_width)
    keys = selected[:, :, :local_width].reshape(groups, NEIGH * span, heads_here, head_dim)
    values = selected[:, :, local_width:].reshape(groups, NEIGH * span, heads_here, head_dim)
    queries = queries.astype(jnp.bfloat16).reshape(groups, GROUP, heads_here, head_dim)
    scores = (
        jnp.einsum("cqhd,ckhd->chqk", queries, keys, preferred_element_type=jnp.float32) * scale
    )
    top = jnp.max(scores, axis=-1, keepdims=True)
    weights = jnp.exp(scores - top)
    probs = (weights / jnp.sum(weights, axis=-1, keepdims=True)).astype(jnp.bfloat16)
    attended = jnp.einsum(
        "chqk,ckhd->cqhd", probs, values, preferred_element_type=jnp.float32
    ).astype(jnp.bfloat16)
    attended = attended.reshape(tok_rows, local_width)
    column_block = lax.all_to_all(w_out, "an", split_axis=1, concat_axis=0, tiled=True)
    rows = column_block
    summed = jnp.dot(
        lax.all_gather(attended, "an", axis=1, tiled=True), rows, preferred_element_type=jnp.float32
    )
    return summed.astype(jnp.bfloat16)


def solution(mesh):
    placed = (
        P("sa", "an"),
        P(None, "an"),
        P(None, "an"),
        P(None, "an"),
        P("an", None),
        P(),
        P(),
        P(("sa", "an"), None, None),
        P("sa"),
    )
    return jax.shard_map(
        shards, mesh=mesh, in_specs=placed, out_specs=P("sa", "an"), check_vma=False
    )
```

profile of v0, /device:TPU:0, one launch (start us, length us, event | category | flops | bytes accessed | tf_op | source)
XLA Modules:
  0.0 301.6 jit_solution(9796901206107320811)
XLA Ops:
  6.5 0.0 copy-start
  6.5 0.0 all-gather.4.cloned.1.call-start
  6.5 0.8 fusion.66
  7.4 0.4 and_reduce_fusion
  7.8 0.2 reduce_window_sum.11
  7.9 0.1 select_reduce_fusion
  8.0 0.1 fusion.62
  8.2 0.0 copy-done
  8.2 0.6 gather_fusion
  8.8 0.2 multiply_reduce_fusion.1
  9.0 0.2 fusion.54
  9.1 0.0 copy-start.4
  9.1 0.0 copy-start.5
  9.2 17.1 %fusion.47 = bf16[256,1024]{1,0:T(8,128)(2,1)} fusion(bf16[4096,1024]{1,0:T(8,128)(2,1)} %param.15, bf16[256,1024]{1,0:T(8,128)(2,1)S(1)} %fusion.54, bf16[1024,4096]{1,0:T(8,128)(2,1)} %param.14, bf16[256,1024]{1,0:T(8,128)(2,1)S(1)} %bitcast.39), kind=kOutput, calls=%fused_computation.63 | convolution fusion | flops 4363911168 | bytes 18350080 | tf_op jit(solution)/shard_map/dot_general | solution.py:20
  26.3 0.0 all-gather.4.cloned.1.call-update
  26.3 0.0 all-gather.6.cloned.1.call-start
  26.3 0.7 all-gather.6.cloned.1.call-update
  27.0 0.2 all-gather.8.cloned.1.call-start
  27.3 0.7 gather_fusion.1
  28.0 71.9 %all-gather.4.cloned.1.call-done = bf16[4096,1024]{1,0:T(8,128)(2,1)} async-done(((bf16[256,1024]{1,0:T(8,128)(2,1)}), bf16[4096,1024]{1,0:T(8,128)(2,1)}) %all-gather.4.cloned.1.call-update) | async-done | bytes 8388624 | tf_op jit(solution)/shard_map/all_gather | solution.py:64
  99.9 0.0 copy-done.4
  99.9 0.0 copy-done.5
  99.9 9.6 %convolution_convert_fusion = bf16[4096,512]{1,0:T(8,128)(2,1)} fusion(bf16[4096,1024]{1,0:T(8,128)(2,1)} %all-gather.4.cloned.1.call-done, bf16[1024,256]{1,0:T(8,128)(2,1)S(1)} %copy-done.4, bf16[1024,256]{1,0:T(8,128)(2,1)S(1)} %copy-done.5), kind=kOutput, calls=%fused_computation.5 | convolution fusion | flops 4299161600 | bytes 13631488 | tf_op jit(solution)/shard_map/dot_general | solution.py:63
  109.5 5.2 %gather_fusion.2 = bf16[32,128,512]{2,1,0:T(8,128)(2,1)} fusion(bf16[32,128,512]{2,1,0:T(8,128)(2,1)} %bitcast.40, s32[1024]{0:T(1024)S(1)} %pad_clamp_fusion), kind=kCustom, calls=%fused_computation.2 | custom fusion | bytes 8388736 | tf_op jit(solution)/shard_map/gather | solution.py:70
  114.6 4.0 %fusion.104 = (bf16[16,256,256]{2,1,0:T(8,128)(2,1)}, bf16[16,256,256]{2,1,0:T(8,128)(2,1)S(1)}) fusion(bf16[16,256,512]{2,1,0:T(8,128)(2,1)} %bitcast.35), kind=kLoop, calls=%fused_computation.137 | loop fusion | bytes 8388608 | tf_op jit(solution)/shard_map/slice | solution.py:71
  118.7 2.4 copy.23
  121.1 2.8 copy.24
  123.9 55.0 %all-gather.6.cloned.1.call-done = bf16[1024,4096]{1,0:T(8,128)(2,1)} async-done(((bf16[1024,256]{1,0:T(8,128)(2,1)}), bf16[1024,4096]{1,0:T(8,128)(2,1)}) %all-gather.6.cloned.1.call-update) | async-done | bytes 8388624 | tf_op jit(solution)/shard_map/all_gather | solution.py:56
  179.0 6.3 %convolution_convert_fusion.3 = bf16[1024,256]{1,0:T(8,128)(2,1)S(1)} fusion(bf16[1024,4096]{1,0:T(8,128)(2,1)} %all-gather.6.cloned.1.call-done, bf16[4096,256]{1,0:T(8,128)(2,1)} %param.10), kind=kOutput, calls=%fused_computation.62 | convolution fusion | flops 2147745792 | bytes 11010048 | tf_op jit(solution)/shard_map/dot_general | solution.py:55
  185.3 0.1 reshape.115
  185.4 0.4 fusion.56
  185.8 0.0 copy-start.3
  185.8 0.8 fusion.105
  186.6 0.6 copy-done.3
  187.2 0.0 copy-start.2
  187.2 6.0 %fusion.50 = bf16[16,64,2,128]{3,1,2,0:T(8,128)(2,1)S(1)} fusion(bf16[16,256,2,128]{1,3,2,0:T(8,128)(2,1)} %bitcast.41, f32[16,2,64]{2,1,0:T(2,128)S(1)} %fusion.105, f32[16,2,64,256]{3,2,1,0:T(8,128)} %copy-done.3), kind=kOutput, calls=%fused_computation.64 | convolution fusion | flops 136579328 | bytes 4726784 | tf_op jit(solution)/shard_map/chqk,ckhd->cqhd/dot_general | solution.py:80
  193.2 0.6 copy.28
  193.8 0.9 copy.37
  194.6 0.0 all-gather.8.cloned.1.call-update
  194.7 0.0 copy-done.2
  194.7 2.5 copy.29
  197.2 40.1 %all_to_all.19 = bf16[256,16,256]{0,2,1:T(8,128)(2,1)S(1)} all-to-all(bf16[256,16,256]{0,2,1:T(8,128)(2,1)} %bitcast.38), channel_id=1, replica_groups=mesh['sa'=8,'an'=16] {'an'}, dimensions={1} | all-to-all | bytes 4194304 | tf_op jit(solution)/shard_map/all_to_all | solution.py:84
  237.3 2.4 copy.30
  239.7 48.1 %all-gather.8.cloned.1.call-done = bf16[1024,4096]{1,0:T(8,128)(2,1)} async-done(((bf16[1024,256]{1,0:T(8,128)(2,1)}), bf16[1024,4096]{1,0:T(8,128)(2,1)}) %all-gather.8.cloned.1.call-update) | async-done | bytes 8388624 | tf_op jit(solution)/shard_map/all_gather | solution.py:87
  287.9 0.0 copy-start.1
  287.9 7.2 %convolution_convert_fusion.1 = bf16[1024,256]{1,0:T(8,128)(2,1)} fusion(bf16[1024,4096]{1,0:T(8,128)(2,1)} %all-gather.8.cloned.1.call-done, bf16[4096,256]{1,0:T(8,128)(2,1)} %bitcast.42), kind=kOutput, calls=%fused_computation.60 | convolution fusion | flops 2147745792 | bytes 11010048 | tf_op jit(solution)/shard_map/dot_general | solution.py:86
  295.1 0.0 copy-done.1
  (10 shorter events, 0.1 us)
Async XLA Ops:
  6.5 1.6 copy-start
  6.5 93.3 %all-gather.4.cloned.1.call-start = ((), (), s32[]{:S(2)}) async-start(), calls=%async_computation.1 | async-start | bytes 8912896 | tf_op jit(solution)/shard_map/all_gather | solution.py:64
  9.1 90.7 %copy-start.4 = (bf16[1024,256]{1,0:T(8,128)(2,1)S(1)}, bf16[1024,256]{1,0:T(8,128)(2,1)}, u32[]{:S(2)}) copy-start(bf16[1024,256]{1,0:T(8,128)(2,1)} %param.12) | copy-start | bytes 1572868
  9.1 90.7 %copy-start.5 = (bf16[1024,256]{1,0:T(8,128)(2,1)S(1)}, bf16[1024,256]{1,0:T(8,128)(2,1)}, u32[]{:S(2)}) copy-start(bf16[1024,256]{1,0:T(8,128)(2,1)} %param.11) | copy-start | bytes 1572868
  26.3 152.7 %all-gather.6.cloned.1.call-start = ((), (), s32[]{:S(2)}) async-start(), calls=%async_computation.2 | async-start | bytes 8912896 | tf_op jit(solution)/shard_map/all_gather | solution.py:56
  27.0 260.8 %all-gather.8.cloned.1.call-start = ((), (), s32[]{:S(2)}) async-start(), calls=%async_computation.3 | async-start | bytes 8912896 | tf_op jit(solution)/shard_map/all_gather | solution.py:87
  185.8 1.4 copy-start.3
  187.2 7.5 %copy-start.2 = (bf16[256,4096]{1,0:T(8,128)(2,1)S(1)}, bf16[256,4096]{1,0:T(8,128)(2,1)}, u32[]{:S(2)}) copy-start(bf16[256,4096]{1,0:T(8,128)(2,1)} %param.13) | copy-start | bytes 6291460
  287.9 7.3 %copy-start.1 = (bf16[8,128,1024]{2,1,0:T(8,128)(2,1)S(1)}, bf16[8,128,1024]{2,1,0:T(8,128)(2,1)}, u32[]{:S(2)}) copy-start(bf16[8,128,1024]{2,1,0:T(8,128)(2,1)} %param.16) | copy-start | bytes 6291460
Sparse Core Ops, SparseCore 0:
  26.4 73.4 all-gather.3
  102.0 76.9 all-gather.5
  194.8 93.0 all-gather.7
where the time goes:
time: 302 us
  waiting for transfers between devices  176 us (58%)
  matrix products  46.7 us (15%)
  blocking collectives  40.1 us (13%)
  local copies, waits for them, and re-layouts  22.9 us (8%)
  between operations  13.2 us (4%)
    all_gather x1, waiting for transfers between devices, shards(): lax.all_gather(encoded, 'an', axis=0, tiled=True)  71.9 us
    all_gather x1, waiting for transfers between devices, shards(): lax.all_gather(decoder_states, 'an', axis=1, tiled=True)  55 us
    all_gather x1, waiting for transfers between devices, shards(): lax.all_gather(attended, 'an', axis=1, tiled=True)  48.1 us
    all_to_all x1, blocking collectives, shards(): lax.all_to_all(w_out, 'an', split_axis=1, concat_axis=0, tiled=True)  40.1 us
    dot_general x1, matrix products, encode(): jnp.dot(hidden, enc_down, preferred_element_type=jnp.float32)  17.1 us
    dot_general x1, matrix products, shards(): jnp.dot(lax.all_gather(encoded, 'an', axis=0, tiled=True), both_weights,...  9.59 us
    dot_general x1, matrix products, shards(): jnp.dot(lax.all_gather(attended, 'an', axis=1, tiled=True), rows, preferr...  7.25 us
    slice x2, local copies, waits for them, and re-layouts, shards(): selected[:, :, :local_width]  6.87 us
  transfers between devices with their start and end apart: 3, of which 3 were waited for; matrix products, arithmetic and copies ran while one was open for 10% of the time, Pallas kernels for 0%

commit v1 on v0

--- a/solution.py
+++ b/solution.py
@@ -53,7 +53,9 @@
     local_of_slot = jnp.sum(jnp.where(chosen_mask, local_range[:, None], 0), axis=0)
     rows = w_query
     queries = jnp.dot(
-        lax.all_gather(decoder_states, "an", axis=1, tiled=True),
+        jnp.concatenate(
+            lax.all_to_all(jnp.stack([decoder_states] * lax.axis_size("an")), "an", 0, 0), axis=1
+        ),
         rows,
         preferred_element_type=jnp.float32,
     )

time: 302 us -> 356 us (1.18)
  waiting for transfers between devices: 176 us -> 214 us
  starting transfers between devices: 0.26 us -> 8.57 us
  local copies, waits for them, and re-layouts: 22.9 us -> 27 us
    all_to_all x0 -> x1, waiting for transfers between devices: none -> 153 us  [shards(): lax.all_to_all(jnp.stack([decoder_states] * lax.axis_size('an')), 'an', 0...]
    all_gather x1, waiting for transfers between devices: 71.9 us -> 13 us  [shards(): lax.all_gather(encoded, 'an', axis=0, tiled=True)]
    all_gather x1 -> x0, waiting for transfers between devices: 55 us -> none  [shards(): lax.all_gather(decoder_states, 'an', axis=1, tiled=True)]
    all_to_all x0 -> x1, starting transfers between devices: none -> 8.34 us  [shards(): lax.all_to_all(jnp.stack([decoder_states] * lax.axis_size('an')), 'an', 0...]
    another operation x0 -> x1, local copies, waits for them, and re-layouts: none -> 4.3 us  [shards(): jnp.stack([decoder_states] * lax.axis_size('an'))]
  transfers between devices with their start and end apart: 3 -> 3, of which waited for: 3 -> 3; matrix products, arithmetic and copies ran while one was open for 10% -> 5% of each run, Pallas kernels for 0% -> 0%
where the time goes in v1:
time: 356 us
  waiting for transfers between devices  214 us (60%)
  matrix products  46.7 us (13%)
  blocking collectives  43.1 us (12%)
  local copies, waits for them, and re-layouts  27 us (8%)
  between operations  13.5 us (4%)
  starting transfers between devices  8.57 us (2%)
    all_to_all x1, waiting for transfers between devices, shards(): lax.all_to_all(jnp.stack([decoder_states] * lax.axis_size('an')), 'an', 0...  153 us
    all_gather x1, waiting for transfers between devices, shards(): lax.all_gather(attended, 'an', axis=1, tiled=True)  47.9 us
    all_to_all x1, blocking collectives, shards(): lax.all_to_all(w_out, 'an', split_axis=1, concat_axis=0, tiled=True)  43.1 us
    dot_general x1, matrix products, encode(): jnp.dot(hidden, enc_down, preferred_element_type=jnp.float32)  17.1 us
    all_gather x1, waiting for transfers between devices, shards(): lax.all_gather(encoded, 'an', axis=0, tiled=True)  13 us
    dot_general x1, matrix products, shards(): jnp.dot(lax.all_gather(encoded, 'an', axis=0, tiled=True), both_weights,...  10.1 us
    all_to_all x1, starting transfers between devices, shards(): lax.all_to_all(jnp.stack([decoder_states] * lax.axis_size('an')), 'an', 0...  8.34 us
    dot_general x1, matrix products, shards(): jnp.dot(lax.all_gather(attended, 'an', axis=1, tiled=True), rows, preferr...  7.25 us
  transfers between devices with their start and end apart: 3, of which 3 were waited for; matrix products, arithmetic and copies ran while one was open for 5% of the time, Pallas kernels for 0%

profile of v1, /device:TPU:0, one launch (start us, length us, event | category | flops | bytes accessed | tf_op | source)
XLA Modules:
  0.0 355.9 jit_solution(6922819117377517457)
XLA Ops:
  6.5 0.0 copy-start
  6.5 0.0 all-gather.3.cloned.1.call-start
  6.5 0.8 fusion.66
  7.4 0.4 and_reduce_fusion
  7.8 0.2 reduce_window_sum.11
  7.9 0.1 select_reduce_fusion
  8.0 0.1 fusion.62
  8.2 0.0 copy-done
  8.2 0.6 gather_fusion
  8.8 0.2 multiply_reduce_fusion.1
  9.0 0.2 fusion.54
  9.1 0.0 copy-start.5
  9.1 17.1 %fusion.47 = bf16[256,1024]{1,0:T(8,128)(2,1)} fusion(bf16[4096,1024]{1,0:T(8,128)(2,1)} %param.15, bf16[256,1024]{1,0:T(8,128)(2,1)S(1)} %fusion.54, bf16[1024,4096]{1,0:T(8,128)(2,1)} %param.14, bf16[256,1024]{1,0:T(8,128)(2,1)S(1)} %bitcast.42), kind=kOutput, calls=%fused_computation.63 | convolution fusion | flops 4363911168 | bytes 18350080 | tf_op jit(solution)/shard_map/dot_general | solution.py:20
  26.2 0.0 all-gather.3.cloned.1.call-update
  26.2 0.0 copy-done.5
  26.2 0.2 copy.26
  26.5 4.3 %stack.2 = bf16[16,1024,256]{1,2,0:T(8,128)(2,1)} broadcast(bf16[1024,256]{0,1:T(8,128)(2,1)S(1)} %copy.26), dimensions={1,2} | broadcast | bytes 8912896 | tf_op jit(solution)/shard_map/stack | solution.py:57
  30.8 0.0 copy-start.4
  30.8 8.3 %all-to-all-start = ((bf16[16,1024,256]{1,2,0:T(8,128)(2,1)}), bf16[16,1024,256]{1,2,0:T(8,128)(2,1)}, u32[]{:S(2)}, u32[]{:S(2)}) async-start(bf16[16,1024,256]{1,2,0:T(8,128)(2,1)} %stack.2), calls=%async_computation | async-start | bytes 16777216 | tf_op jit(solution)/shard_map/all_to_all | solution.py:57
  39.1 0.2 all-gather.5.cloned.1.call-start
  39.3 0.7 gather_fusion.1
  40.1 153.4 %all-to-all-done = bf16[16,1024,256]{1,2,0:T(8,128)(2,1)} async-done(((bf16[16,1024,256]{1,2,0:T(8,128)(2,1)}), bf16[16,1024,256]{1,2,0:T(8,128)(2,1)}, u32[]{:S(2)}, u32[]{:S(2)}) %all-to-all-start) | async-done | bytes 8388640 | tf_op jit(solution)/shard_map/all_to_all | solution.py:57
  193.5 0.0 copy-done.4
  193.5 5.8 %convolution_convert_fusion.3 = bf16[1024,256]{1,0:T(8,128)(2,1)S(1)} fusion(bf16[1024,4096]{0,1:T(8,128)(2,1)} %bitcast.8, bf16[4096,256]{1,0:T(8,128)(2,1)S(1)} %copy-done.4), kind=kOutput, calls=%fused_computation.62 | convolution fusion | flops 2147745792 | bytes 11010048 | tf_op jit(solution)/shard_map/dot_general | solution.py:55
  199.3 0.1 reshape.125
  199.4 13.0 %all-gather.3.cloned.1.call-done = bf16[4096,1024]{1,0:T(8,128)(2,1)} async-done(((bf16[256,1024]{1,0:T(8,128)(2,1)}), bf16[4096,1024]{1,0:T(8,128)(2,1)}) %all-gather.3.cloned.1.call-update) | async-done | bytes 8388624 | tf_op jit(solution)/shard_map/all_gather | solution.py:66
  212.4 10.1 %convolution_convert_fusion = bf16[4096,512]{1,0:T(8,128)(2,1)} fusion(bf16[4096,1024]{1,0:T(8,128)(2,1)} %all-gather.3.cloned.1.call-done, bf16[1024,256]{1,0:T(8,128)(2,1)} %param.12, bf16[1024,256]{1,0:T(8,128)(2,1)} %param.11), kind=kOutput, calls=%fused_computation.5 | convolution fusion | flops 4299161600 | bytes 13631488 | tf_op jit(solution)/shard_map/dot_general | solution.py:65
  222.5 4.9 %gather_fusion.2 = bf16[32,128,512]{2,1,0:T(8,128)(2,1)} fusion(bf16[32,128,512]{2,1,0:T(8,128)(2,1)} %bitcast.43, s32[1024]{0:T(1024)S(1)} %pad_clamp_fusion), kind=kCustom, calls=%fused_computation.2 | custom fusion | bytes 8388736 | tf_op jit(solution)/shard_map/gather | solution.py:72
  227.4 4.0 %fusion.104 = (bf16[16,256,256]{2,1,0:T(8,128)(2,1)}, bf16[16,256,256]{2,1,0:T(8,128)(2,1)S(1)}) fusion(bf16[16,256,512]{2,1,0:T(8,128)(2,1)} %bitcast.38), kind=kLoop, calls=%fused_computation.137 | loop fusion | bytes 8388608 | tf_op jit(solution)/shard_map/slice | solution.py:73
  231.4 2.4 copy.25
  233.8 2.8 copy.27
  236.6 0.4 fusion.56
  237.1 0.0 copy-start.3
  237.1 0.8 fusion.105
  237.8 0.5 copy-done.3
  238.4 0.0 copy-start.2
  238.4 6.0 %fusion.50 = bf16[16,64,2,128]{3,1,2,0:T(8,128)(2,1)S(1)} fusion(bf16[16,256,2,128]{1,3,2,0:T(8,128)(2,1)} %bitcast.44, f32[16,2,64]{2,1,0:T(2,128)S(1)} %fusion.105, f32[16,2,64,256]{3,2,1,0:T(8,128)} %copy-done.3), kind=kOutput, calls=%fused_computation.64 | convolution fusion | flops 136579328 | bytes 4726784 | tf_op jit(solution)/shard_map/chqk,ckhd->cqhd/dot_general | solution.py:82
  244.4 0.5 copy.31
  244.9 0.9 copy.40
  245.8 0.0 all-gather.5.cloned.1.call-update
  245.8 0.0 copy-done.2
  245.9 2.5 copy.32
  248.4 43.1 %all_to_all.24 = bf16[256,16,256]{0,2,1:T(8,128)(2,1)S(1)} all-to-all(bf16[256,16,256]{0,2,1:T(8,128)(2,1)} %bitcast.41), channel_id=1, replica_groups=mesh['sa'=8,'an'=16] {'an'}, dimensions={1} | all-to-all | bytes 4194304 | tf_op jit(solution)/shard_map/all_to_all | solution.py:86
  291.5 2.4 copy.33
  293.9 47.9 %all-gather.5.cloned.1.call-done = bf16[1024,4096]{1,0:T(8,128)(2,1)} async-done(((bf16[1024,256]{1,0:T(8,128)(2,1)}), bf16[1024,4096]{1,0:T(8,128)(2,1)}) %all-gather.5.cloned.1.call-update) | async-done | bytes 8388624 | tf_op jit(solution)/shard_map/all_gather | solution.py:89
  341.8 0.0 copy-start.1
  341.8 7.2 %convolution_convert_fusion.1 = bf16[1024,256]{1,0:T(8,128)(2,1)} fusion(bf16[1024,4096]{1,0:T(8,128)(2,1)} %all-gather.5.cloned.1.call-done, bf16[4096,256]{1,0:T(8,128)(2,1)} %bitcast.45), kind=kOutput, calls=%fused_computation.60 | convolution fusion | flops 2147745792 | bytes 11010048 | tf_op jit(solution)/shard_map/dot_general | solution.py:88
  349.0 0.0 copy-done.1
  (10 shorter events, 0.1 us)
Async XLA Ops:
  6.5 1.6 copy-start
  6.5 205.9 %all-gather.3.cloned.1.call-start = ((), (), s32[]{:S(2)}) async-start(), calls=%async_computation.2 | async-start | bytes 8912896 | tf_op jit(solution)/shard_map/all_gather | solution.py:66
  9.1 17.1 %copy-start.5 = (bf16[1024,256]{1,0:T(8,128)(2,1)S(1)}, bf16[1024,256]{1,0:T(8,128)(2,1)}, u32[]{:S(2)}) copy-start(bf16[1024,256]{1,0:T(8,128)(2,1)} %param.9) | copy-start | bytes 1572868
  30.8 162.7 %copy-start.4 = (bf16[4096,256]{1,0:T(8,128)(2,1)S(1)}, bf16[4096,256]{1,0:T(8,128)(2,1)}, u32[]{:S(2)}) copy-start(bf16[4096,256]{1,0:T(8,128)(2,1)} %param.10) | copy-start | bytes 6291460
  30.8 162.7 %all-to-all-start = ((bf16[16,1024,256]{1,2,0:T(8,128)(2,1)}), bf16[16,1024,256]{1,2,0:T(8,128)(2,1)}, u32[]{:S(2)}, u32[]{:S(2)}) async-start(bf16[16,1024,256]{1,2,0:T(8,128)(2,1)} %stack.2), calls=%async_computation | async-start | bytes 16777216 | tf_op jit(solution)/shard_map/all_to_all | solution.py:57
  39.1 302.7 %all-gather.5.cloned.1.call-start = ((), (), s32[]{:S(2)}) async-start(), calls=%async_computation.3 | async-start | bytes 8912896 | tf_op jit(solution)/shard_map/all_gather | solution.py:89
  237.1 1.3 copy-start.3
  238.4 7.5 %copy-start.2 = (bf16[256,4096]{1,0:T(8,128)(2,1)S(1)}, bf16[256,4096]{1,0:T(8,128)(2,1)}, u32[]{:S(2)}) copy-start(bf16[256,4096]{1,0:T(8,128)(2,1)} %param.13) | copy-start | bytes 6291460
  341.8 7.3 %copy-start.1 = (bf16[8,128,1024]{2,1,0:T(8,128)(2,1)S(1)}, bf16[8,128,1024]{2,1,0:T(8,128)(2,1)}, u32[]{:S(2)}) copy-start(bf16[8,128,1024]{2,1,0:T(8,128)(2,1)} %param.16) | copy-start | bytes 6291460
Sparse Core Ops, SparseCore 0:
  26.4 186.0 all-gather.2
  246.0 95.7 all-gather.4
